TPU v7x, 32 devices: a whole 2x2x4 slice. The times are simulated.
32 devices in a mesh: section: 2 (over core), seq: 4 (over y, x), head: 4 (over z).
Axes of the slice: x: 2, y: 2, z: 4, core: 2. Of those that a mesh axis runs over, the one named last changes fastest.
Arguments:
- x_in: bfloat16 [2, 1024, 8192], P('section', 'seq', 'head'), may hold values from -6 to 6
- b_in: bfloat16 [2, 1024, 2048], P('section', 'seq', 'head'), may hold values from -6 to 6
- c_in: bfloat16 [2, 1024, 2048], P('section', 'seq', 'head'), may hold values from -6 to 6
- z_in: bfloat16 [2, 1024, 8192], P('section', 'seq', 'head'), may hold values from -6 to 6
- dt_raw: float32 [2, 128, 1024], P('section', 'head', 'seq'), may hold values from -5 to 5
- conv_x: float32 [2, 4, 8192], P('section', None, 'head'), may hold values from -3 to 3
- conv_b: float32 [2, 4, 2048], P('section', None, 'head'), may hold values from -3 to 3
- conv_c: float32 [2, 4, 2048], P('section', None, 'head'), may hold values from -3 to 3
- a_rate: float32 [2, 128], P('section', 'head'), may hold values from 0.0001 to 1
- dt_bias: float32 [2, 128], P('section', 'head'), may hold values from -3 to -0.5
- skip_d: float32 [2, 128], P('section', 'head'), may hold values from 0.5 to 2
- norm_gain: float32 [2, 8192], P('section', 'head'), may hold values from 0.25 to 1.75
- out_weight: bfloat16 [2, 8192, 8192], P('section', 'head', 'seq'), may hold values from -0.0625 to 0.0625
Outputs:
- mixed: bfloat16 [2, 1024, 8192], P('section', ('seq', 'head'))
All inputs are finite; a program needn't handle non-finite values.
Results may differ from a plain program's by a relative error of at most 0.007.
Values may be sent and summed in bfloat16 or wider, within the bound.
A program may use at most 128 MiB of HBM per device.

v0:
```python
import jax
import jax.numpy as jnp
from jax import lax
from jax.sharding import PartitionSpec as P

N = 256
epsilon = 1e-05


def passed_along(block, axis, distance):
    devices = range(lax.axis_size(axis))
    route = [(i - distance, i) for i in devices if i - distance in devices]
    return lax.ppermute(block, axis, route)


def entering(decay, block, axis):
    size, place = (lax.axis_size(axis), lax.axis_index(axis))
    decays = lax.all_gather(decay, axis)
    blocks = lax.all_gather(block.astype(jnp.bfloat16), axis)
    carried = jnp.zeros_like(block)
    for k in range(size - 1):
        after = decays[k][:, :, None, None] * carried + blocks[k].astype(jnp.float32)
        carried = jnp.where(k < place, after, carried)
    return carried


def passed_along_2(block, axis, distance):
    devices = range(lax.axis_size(axis))
    route = [((i - distance) % len(devices), i) for i in devices]
    return lax.ppermute(block, axis, route)


def conv_silu(padded, kernel, length):
    kernel_taps = kernel.shape[0]
    summed = jnp.zeros((length, padded.shape[1]), jnp.float32)
    for offset in range(kernel_taps):
        summed = summed + kernel[offset] * padded[offset : offset + length].astype(jnp.float32)
    return jax.nn.silu(summed).astype(jnp.bfloat16)


def per_device(
    x_in,
    b_in,
    c_in,
    z_in,
    dt_raw,
    conv_x,
    conv_b,
    conv_c,
    a_rate,
    dt_bias,
    skip_d,
    norm_gain,
    out_weight,
):
    x_local = x_in[0]
    b_local = b_in[0]
    c_local = c_in[0]
    length = x_local.shape[0]
    kernel_taps = conv_x.shape[1]
    x_cols = x_local.shape[1]
    b_cols = b_local.shape[1]
    edge_rows = jnp.concatenate(
        [
            x_local[length - kernel_taps + 1 :],
            b_local[length - kernel_taps + 1 :],
            c_local[length - kernel_taps + 1 :],
        ],
        axis=1,
    )
    before = passed_along(edge_rows, "seq", 1)
    x_conv = conv_silu(jnp.concatenate([before[:, :x_cols], x_local], axis=0), conv_x[0], length)
    b_conv = conv_silu(
        jnp.concatenate([before[:, x_cols : x_cols + b_cols], b_local], axis=0), conv_b[0], length
    )
    c_conv = conv_silu(
        jnp.concatenate([before[:, x_cols + b_cols :], c_local], axis=0), conv_c[0], length
    )
    head_count = dt_raw.shape[1]
    group_count = b_cols // N
    per_group = head_count // group_count
    head_dim = x_cols // head_count
    step_size = jax.nn.softplus(dt_raw[0] + dt_bias[0][:, None])
    log_decay = jnp.cumsum(-a_rate[0][:, None] * step_size, axis=1)
    x_groups = x_conv.reshape(length, group_count, per_group, head_dim)
    b_groups = b_conv.reshape(length, group_count, N)
    c_groups = c_conv.reshape(length, group_count, N)
    log_groups = log_decay.reshape(group_count, per_group, length)
    step_groups = step_size.reshape(group_count, per_group, length)
    scores = jnp.einsum("tgn,ugn->gtu", c_groups, b_groups, preferred_element_type=jnp.float32)
    causal = jnp.arange(length)[:, None] >= jnp.arange(length)[None, :]
    spread_log = log_groups[:, :, :, None] - log_groups[:, :, None, :]
    damping = jnp.where(causal, jnp.exp(jnp.minimum(spread_log, 0.0)), 0.0)
    weights = (damping * step_groups[:, :, None, :] * scores[:, None]).astype(jnp.bfloat16)
    inside = jnp.einsum("gjtu,ugjp->tgjp", weights, x_groups, preferred_element_type=jnp.float32)
    to_end = jnp.exp(log_groups[:, :, -1:] - log_groups) * step_groups
    x_weighted = (
        x_groups.astype(jnp.float32) * jnp.transpose(to_end, (2, 0, 1))[..., None]
    ).astype(jnp.bfloat16)
    block_sum = jnp.einsum(
        "ugjp,ugn->gjpn", x_weighted, b_groups, preferred_element_type=jnp.float32
    )
    block_decay = jnp.exp(log_groups[:, :, -1])
    carried = entering(block_decay, block_sum, "seq")
    carried_b = carried.astype(jnp.bfloat16)
    outside = jnp.einsum("tgn,gjpn->tgjp", c_groups, carried_b, preferred_element_type=jnp.float32)
    outside = outside * jnp.transpose(jnp.exp(log_groups), (2, 0, 1))[..., None]
    skip_term = skip_d[0].reshape(group_count, per_group)
    out_ssm = inside + outside + skip_term[None, :, :, None] * x_groups.astype(jnp.float32)
    gate_act = jax.nn.silu(z_in[0].astype(jnp.float32)).reshape(
        length, group_count, per_group * head_dim
    )
    gated = out_ssm.reshape(length, group_count, per_group * head_dim) * gate_act
    inverse_rms = lax.rsqrt(jnp.mean(gated * gated, axis=2, keepdims=True) + epsilon)
    hidden = ((gated * inverse_rms).reshape(length, x_cols) * norm_gain[0]).astype(jnp.bfloat16)
    local_weight = out_weight[0]
    terms = jnp.dot(
        lax.all_gather(hidden, "seq", axis=0, tiled=True),
        local_weight,
        preferred_element_type=jnp.float32,
    )
    shards = lax.axis_size("seq")
    terms = terms.astype(jnp.bfloat16).reshape(shards, length, local_weight.shape[1])
    summed = lax.psum_scatter(terms, "head", scatter_dimension=1, tiled=True)
    spread = lax.all_to_all(summed, "seq", split_axis=0, concat_axis=2, tiled=True)
    mixed = spread.reshape(spread.shape[1], spread.shape[2])
    passed = passed_along_2(mixed, "section", 1)
    return passed[None]


def solution(mesh):
    return jax.shard_map(
        per_device,
        mesh=mesh,
        in_specs=(
            P("section", "seq", "head"),
            P("section", "seq", "head"),
            P("section", "seq", "head"),
            P("section", "seq", "head"),
            P("section", "head", "seq"),
            P("section", None, "head"),
            P("section", None, "head"),
            P("section", None, "head"),
            P("section", "head"),
            P("section", "head"),
            P("section", "head"),
            P("section", "head"),
            P("section", "head", "seq"),
        ),
        out_specs=P("section", ("seq", "head"), None),
        check_vma=False,
    )
```

profile of v0, /device:TPU:0, one launch (start us, length us, event | category | flops | bytes accessed | tf_op | source)
XLA Modules:
  0.0 265.6 jit_solution(9218574246040160207)
XLA Ops:
  6.5 0.9 slice_bitcast_fusion
  8.1 4.9 %collective-permute-start = (bf16[3,3072]{1,0:T(4,128)(2,1)S(1)}, bf16[3,3072]{1,0:T(4,128)(2,1)S(1)}, u32[]{:S(2)}, u32[]{:S(2)}) collective-permute-start(bf16[3,3072]{1,0:T(4,128)(2,1)S(1)} %pad_maximum_fusion.3), channel_id=1, source_target_pairs={{0,4},{4,8},{8,12},{1,5},{5,9},{9,13},{2,6},{6,10},{10,14},{3,7},{... | collective-permute-start | bytes 55304 | tf_op jit(solution)/shard_map/ppermute | solution.py:13
  14.2 1.3 reduce.9
  18.2 0.9 fusion.50
  19.2 1.4 multiply_bitcast_fusion
  20.6 0.9 fusion.53
  21.4 1.9 multiply_convert_fusion.5
  23.5 1.5 multiply_convert_fusion.2
  25.5 1.4 convolution_convert_fusion
  27.8 1.6 copy.67
  29.4 8.1 %all-gather = f32[8,16,1]{1,2,0:T(1,128)S(1)} all-gather(f32[2,16,1]{1,2,0:T(1,128)S(1)} %bitcast.125), channel_id=2, replica_groups=mesh['section'=2,'seq'=4,'head'=4] {'seq'}, dimensions={0}, use_global_device_ids=true | all-gather | bytes 640 | tf_op jit(solution)/shard_map/all_gather | solution.py:18
  38.2 41.8 %all-gather.7.cloned.1.call-done = bf16[8,16,64,256]{3,2,1,0:T(8,128)(2,1)} async-done(((bf16[2,16,64,256]{3,2,1,0:T(8,128)(2,1)}), bf16[8,16,64,256]{3,2,1,0:T(8,128)(2,1)}) %all-gather.7.cloned.1.call-update) | async-done | bytes 4194320 | tf_op jit(solution)/shard_map/all_gather | solution.py:19
  80.0 3.0 %fusion.31 = f32[2,16,64,256]{3,2,1,0:T(8,128)S(1)} fusion(bf16[8,16,64,256]{3,2,1,0:T(8,128)(2,1)} %all-gather.7.cloned.1.call-done, f32[2,16]{1,0:T(2,128)S(1)} %bitcast.128, f32[2,16]{1,0:T(2,128)S(1)} %bitcast.127, f32[2,16]{1,0:T(2,128)S(1)} %bitcast.126, pred[]{:T(512)S(6)} %gt.11, pred[]{:T(512)S(6)} %gt.10, pred[]{:T(512)S(6)} %gt.9, ...), kind=kOutput, calls=%fused_computation.43 | convolution fusion | flops 274726912 | bytes 5505411 | tf_op jit(solution)/shard_map/tgn,gjpn->tgjp/dot_general | solution.py:106
  83.0 4.5 %multiply_reduce_fusion = (f32[256,2]{0,1:T(2,128)S(1)}, f32[256,2,16,64]{0,3,2,1:T(8,128)}) fusion(f32[256,2,16,64]{0,3,2,1:T(8,128)S(1)} %bitcast.99, bf16[256,2,16,64]{0,3,2,1:T(8,128)(2,1)S(1)} %bitcast.103, f32[2,16]{1,0:T(2,128)S(1)} %mul.316, f32[256,2,16]{0,2,1:T(8,128)S(1)} %copy-done.4, f32[2,16,64,256]{3,2,1,0:T(8,128)S(1)} %fusion.31, ...), kind=kOutput, calls=%fused_computation.33 | convolution fusion | flops 287309312 | bytes 8030336 | tf_op jit(solution)/shard_map/gjtu,ugjp->tgjp/dot_general | solution.py:95
  87.5 1.9 copy.66
  90.2 0.9 copy.79
  91.1 1.8 fusion.26
  92.9 52.7 %all-gather.5.cloned.1.call-done = bf16[1024,2048]{1,0:T(8,128)(2,1)} async-done(((bf16[256,2048]{1,0:T(8,128)(2,1)}), bf16[1024,2048]{1,0:T(8,128)(2,1)}) %all-gather.5.cloned.1.call-update) | async-done | bytes 4194320 | tf_op jit(solution)/shard_map/all_gather | solution.py:118
  145.6 13.8 %fusion.9 = bf16[1024,2048]{1,0:T(8,128)(2,1)} fusion(bf16[1024,2048]{1,0:T(8,128)(2,1)} %all-gather.5.cloned.1.call-done, bf16[1,2048,2048]{2,1,0:T(8,128)(2,1)} %param.25), kind=kOutput, calls=%fused_computation.10 | convolution fusion | flops 8592031744 | bytes 16777216 | tf_op jit(solution)/shard_map/dot_general | solution.py:117
  159.4 77.0 %reduce-scatter.2.cloned.1.call-done = bf16[4,64,2048]{2,1,0:T(8,128)(2,1)} async-done(((bf16[4,256,2048]{2,1,0:T(8,128)(2,1)}), bf16[4,64,2048]{2,1,0:T(8,128)(2,1)}) %reduce-scatter.2.cloned.1.call-update) | async-done | bytes 1048592 | tf_op jit(solution)/shard_map/reduce_scatter | solution.py:124
  236.4 17.6 %all_to_all.15 = bf16[4,64,2048]{2,1,0:T(8,128)(2,1)S(1)} all-to-all(bf16[4,64,2048]{2,1,0:T(8,128)(2,1)} %reduce-scatter.2.cloned.1.call-done), channel_id=1, replica_groups=mesh['section'=2,'seq'=4,'head'=4] {'seq'}, dimensions={0} | all-to-all | bytes 2097152 | tf_op jit(solution)/shard_map/all_to_all | solution.py:125
  254.0 0.8 copy.69
  255.5 2.6 collective-permute-done.1
  258.1 1.0 copy.97
  (57 shorter events, 8.3 us)
Async XLA Ops:
  6.5 16.9 %copy-start.2 = (bf16[1,256,2048]{2,1,0:T(8,128)(2,1)S(1)}, bf16[1,256,2048]{2,1,0:T(8,128)(2,1)}, u32[]{:S(2)}) copy-start(bf16[1,256,2048]{2,1,0:T(8,128)(2,1)} %param.13) | copy-start | bytes 3145732
  6.5 73.5 %all-gather.7.cloned.1.call-start = ((), (), s32[]{:S(2)}) async-start(), calls=%async_computation.4 | async-start | bytes 5242880 | tf_op jit(solution)/shard_map/all_gather | solution.py:19
  8.1 13.3 %collective-permute-start = (bf16[3,3072]{1,0:T(4,128)(2,1)S(1)}, bf16[3,3072]{1,0:T(4,128)(2,1)S(1)}, u32[]{:S(2)}, u32[]{:S(2)}) collective-permute-start(bf16[3,3072]{1,0:T(4,128)(2,1)S(1)} %pad_maximum_fusion.3), channel_id=1, source_target_pairs={{0,4},{4,8},{8,12},{1,5},{5,9},{9,13},{2,6},{6,10},{10,14},{3,7},{... | collective-permute-start | bytes 55304 | tf_op jit(solution)/shard_map/ppermute | solution.py:13
  25.5 1.6 copy-start.7
  25.5 2.3 copy-start
  26.9 10.6 %copy-start.6 = (f32[1,4,512]{2,1,0:T(4,128)S(1)}, f32[1,4,512]{2,1,0:T(4,128)}, u32[]{:S(2)}) copy-start(f32[1,4,512]{2,1,0:T(4,128)} %param.20) | copy-start | bytes 24580
  26.9 10.6 %copy-start.3 = (bf16[1,256,512]{2,1,0:T(8,128)(2,1)S(1)}, bf16[1,256,512]{2,1,0:T(8,128)(2,1)}, u32[]{:S(2)}) copy-start(bf16[1,256,512]{2,1,0:T(8,128)(2,1)} %param.15) | copy-start | bytes 786436
  27.0 118.6 %all-gather.5.cloned.1.call-start = ((), (), s32[]{:S(2)}) async-start(), calls=%async_computation.2 | async-start | bytes 5242880 | tf_op jit(solution)/shard_map/all_gather | solution.py:118
  80.0 3.0 %copy-start.1 = (f32[1,256,2048]{1,2,0:T(8,128)S(1)}, f32[1,256,2048]{1,2,0:T(8,128)}, u32[]{:S(2)}) copy-start(f32[1,256,2048]{1,2,0:T(8,128)} %copy.67) | copy-start | bytes 6291460
  80.0 3.0 %copy-start.4 = (f32[256,2,16]{0,2,1:T(8,128)S(1)}, f32[256,2,16]{0,2,1:T(8,128)}, u32[]{:S(2)}) copy-start(f32[256,2,16]{0,2,1:T(8,128)} %get-tuple-element.7) | copy-start | bytes 98308
  90.2 0.9 copy-start.5
  92.9 143.5 %reduce-scatter.2.cloned.1.call-start = ((), (), s32[]{:S(2)}) async-start(), calls=%async_computation.3 | async-start | bytes 5242880 | tf_op jit(solution)/shard_map/reduce_scatter | solution.py:124
  255.4 2.7 %collective-permute-start.1 = (bf16[64,8192]{1,0:T(8,128)(2,1)S(1)}, bf16[64,8192]{1,0:T(8,128)(2,1)S(1)}, u32[]{:S(2)}, u32[]{:S(2)}) collective-permute-start(bf16[64,8192]{1,0:T(8,128)(2,1)S(1)} %bitcast.104), channel_id=1, source_target_pairs={{16,0},{0,16},{17,1},{1,17},{18,2},{2,18},{19,3},{3,19},{20,4},{4,... | collective-permute-start | bytes 3145736 | tf_op jit(solution)/shard_map/ppermute | solution.py:30
Sparse Core Ops, SparseCore 0:
  27.1 52.8 all-gather.6
  93.0 52.5 all-gather.4
  159.6 76.7 reduce-scatter.1
where the time goes:
time: 266 us
  waiting for transfers between devices  174 us (65%)
  blocking collectives  25.7 us (10%)
  matrix products  22.9 us (9%)
  local copies, waits for them, and re-layouts  13.5 us (5%)
  between operations  13.4 us (5%)
  other arithmetic  11 us (4%)
  starting transfers between devices  5.03 us (2%)
    reduce_scatter x1, waiting for transfers between devices, per_device(): summed = lax.psum_scatter(terms, 'head', scatter_dimension=1, tiled=True)  77 us
    all_gather x1, waiting for transfers between devices, per_device(): lax.all_gather(hidden, 'seq', axis=0, tiled=True)  52.7 us
    all_gather x1, waiting for transfers between devices, entering(): blocks = lax.all_gather(block.astype(jnp.bfloat16), axis)  41.8 us
    all_to_all x1, blocking collectives, per_device(): lax.all_to_all(summed, 'seq', split_axis=0, concat_axis=2, tiled=True)  17.6 us
    dot_general x1, matrix products, per_device(): jnp.dot(lax.all_gather(hidden, 'seq', axis=0, tiled=True), local_weight,...  13.8 us
    all_gather x1, blocking collectives, entering(): decays = lax.all_gather(decay, axis)  8.08 us
  transfers between devices with their start and end apart: 5, of which 4 were waited for; matrix products, arithmetic and copies ran while one was open for 4% of the time, Pallas kernels for 0%

commit v1 on v0

--- a/solution.py
+++ b/solution.py
@@ -5,6 +5,28 @@
 
 N = 256
 epsilon = 1e-05
+
+
+def joined_along(parts, dim):
+    parts = jnp.moveaxis(parts, 0, dim)
+    dims = parts.shape
+    return parts.reshape(*dims[:dim], dims[dim] * dims[dim + 1], *dims[dim + 2 :])
+
+
+def doubled(x, axis):
+    size = lax.axis_size(axis)
+    blocks = x[None]
+    for level in range(size.bit_length() - 1):
+        distance = 1 << level
+        other = lax.ppermute(blocks, axis, [(i, i ^ distance) for i in range(size)])
+        both = jnp.stack([blocks, other])
+        upper = lax.axis_index(axis) >> level & 1
+        blocks = jnp.where(upper == 0, both, both[::-1]).reshape(-1, *x.shape)
+    return blocks
+
+
+def gather_by_bits(array, axis, dim):
+    return joined_along(doubled(array, axis), dim)
 
 
 def passed_along(block, axis, distance):
@@ -115,9 +137,7 @@
     hidden = ((gated * inverse_rms).reshape(length, x_cols) * norm_gain[0]).astype(jnp.bfloat16)
     local_weight = out_weight[0]
     terms = jnp.dot(
-        lax.all_gather(hidden, "seq", axis=0, tiled=True),
-        local_weight,
-        preferred_element_type=jnp.float32,
+        gather_by_bits(hidden, "seq", 0), local_weight, preferred_element_type=jnp.float32
     )
     shards = lax.axis_size("seq")
     terms = terms.astype(jnp.bfloat16).reshape(shards, length, local_weight.shape[1])

time: 266 us -> 295 us (1.11)
  other arithmetic: 11 us -> 22.4 us
  local copies, waits for them, and re-layouts: 13.5 us -> 23.3 us
  waiting for transfers between devices: 174 us -> 182 us
  matrix products: 22.9 us -> 19.7 us
    ppermute x0 -> x2, waiting for transfers between devices: none -> 60.6 us  [doubled(): other = lax.ppermute(blocks, axis, [(i, i ^ distance) for i in range(size)])]
    all_gather x1 -> x0, waiting for transfers between devices: 52.7 us -> none  [per_device(): lax.all_gather(hidden, 'seq', axis=0, tiled=True)]
    mul x1 -> x3, local copies, waits for them, and re-layouts: 0.61 us -> 6.26 us  [per_device(): gated * inverse_rms]
    another operation x3 -> x6, other arithmetic: 0.71 us -> 6.31 us  [the longest x3 5.61 us: doubled(): both = jnp.stack([blocks, other])]
    convert_element_type x1 -> x2, other arithmetic: 1.77 us -> 6.29 us  [per_device(): ((gated * inverse_rms).reshape(length, x_cols) * norm_gain[0]).astype(jnp...]
    reshape x1 -> x2, local copies, waits for them, and re-layouts: 1.92 us -> 5.97 us  [per_device(): out_ssm.reshape(length, group_count, per_group * head_dim) * gate_act]
    dot_general x1, matrix products: 13.8 us -> 10.4 us  [per_device(): jnp.dot(gather_by_bits(hidden, 'seq', 0), local_weight, preferred_element...]
  transfers between devices with their start and end apart: 5 -> 6, of which waited for: 4 -> 5; matrix products, arithmetic and copies ran while one was open for 4% -> 7% of each run, Pallas kernels for 0% -> 0%
where the time goes in v1:
time: 295 us
  waiting for transfers between devices  182 us (62%)
  blocking collectives  25.7 us (9%)
  local copies, waits for them, and re-layouts  23.3 us (8%)
  other arithmetic  22.4 us (8%)
  matrix products  19.7 us (7%)
  between operations  13.7 us (5%)
  starting transfers between devices  7.92 us (3%)
    reduce_scatter x1, waiting for transfers between devices, per_device(): summed = lax.psum_scatter(terms, 'head', scatter_dimension=1, tiled=True)  77 us
    ppermute x2, waiting for transfers between devices, doubled(): other = lax.ppermute(blocks, axis, [(i, i ^ distance) for i in range(size)])  60.6 us
    all_gather x1, waiting for transfers between devices, entering(): blocks = lax.all_gather(block.astype(jnp.bfloat16), axis)  41.8 us
    all_to_all x1, blocking collectives, per_device(): lax.all_to_all(summed, 'seq', split_axis=0, concat_axis=2, tiled=True)  17.6 us
    dot_general x1, matrix products, per_device(): jnp.dot(gather_by_bits(hidden, 'seq', 0), local_weight, preferred_element...  10.4 us
    all_gather x1, blocking collectives, entering(): decays = lax.all_gather(decay, axis)  8.08 us
    convert_element_type x2, other arithmetic, per_device(): ((gated * inverse_rms).reshape(length, x_cols) * norm_gain[0]).astype(jnp...  6.29 us
    mul x3, local copies, waits for them, and re-layouts, per_device(): gated * inverse_rms  6.26 us
  transfers between devices with their start and end apart: 6, of which 5 were waited for; matrix products, arithmetic and copies ran while one was open for 7% of the time, Pallas kernels for 0%

profile of v1, /device:TPU:0, one launch (start us, length us, event | category | flops | bytes accessed | tf_op | source)
XLA Modules:
  0.0 294.7 jit_solution(15944919457631648068)
XLA Ops:
  8.1 4.9 %collective-permute-start = (bf16[3,3072]{1,0:T(4,128)(2,1)S(1)}, bf16[3,3072]{1,0:T(4,128)(2,1)S(1)}, u32[]{:S(2)}, u32[]{:S(2)}) collective-permute-start(bf16[3,3072]{1,0:T(4,128)(2,1)S(1)} %pad_maximum_fusion.5), channel_id=1, source_target_pairs={{0,4},{4,8},{8,12},{1,5},{5,9},{9,13},{2,6},{6,10},{10,14},{3,7},{... | collective-permute-start | bytes 55304 | tf_op jit(solution)/shard_map/ppermute | solution.py:35
  21.4 1.9 multiply_convert_fusion.6
  23.4 1.5 multiply_convert_fusion.3
  27.7 1.6 copy.71
  29.3 8.1 %all-gather = f32[8,16,1]{1,2,0:T(1,128)S(1)} all-gather(f32[2,16,1]{1,2,0:T(1,128)S(1)} %bitcast.132), channel_id=2, replica_groups=mesh['section'=2,'seq'=4,'head'=4] {'seq'}, dimensions={0}, use_global_device_ids=true | all-gather | bytes 640 | tf_op jit(solution)/shard_map/all_gather | solution.py:40
  38.1 41.8 %all-gather.4.cloned.1.call-done = bf16[8,16,64,256]{3,2,1,0:T(8,128)(2,1)} async-done(((bf16[2,16,64,256]{3,2,1,0:T(8,128)(2,1)}), bf16[8,16,64,256]{3,2,1,0:T(8,128)(2,1)}) %all-gather.4.cloned.1.call-update) | async-done | bytes 4194320 | tf_op jit(solution)/shard_map/all_gather | solution.py:41
  80.0 3.0 %fusion.33 = f32[2,16,64,256]{3,2,1,0:T(8,128)S(1)} fusion(bf16[8,16,64,256]{3,2,1,0:T(8,128)(2,1)} %all-gather.4.cloned.1.call-done, f32[2,16]{1,0:T(2,128)S(1)} %bitcast.135, f32[2,16]{1,0:T(2,128)S(1)} %bitcast.134, f32[2,16]{1,0:T(2,128)S(1)} %bitcast.133, pred[]{:T(512)S(6)} %gt.11, pred[]{:T(512)S(6)} %gt.10, pred[]{:T(512)S(6)} %gt.9, ...), kind=kOutput, calls=%fused_computation.50 | convolution fusion | flops 274726912 | bytes 5505411 | tf_op jit(solution)/shard_map/tgn,gjpn->tgjp/dot_general | solution.py:128
  82.9 4.7 %multiply_reduce_fusion = (f32[256,2]{0,1:T(2,128)S(1)}, f32[256,2,16,64]{0,3,2,1:T(8,128)}) fusion(f32[256,2,16,64]{0,3,2,1:T(8,128)S(1)} %bitcast.106, bf16[256,2,16,64]{0,3,2,1:T(8,128)(2,1)S(1)} %bitcast.109, f32[2,16]{1,0:T(2,128)S(1)} %mul.360, f32[256,2,16]{0,2,1:T(8,128)S(1)} %copy-done.6, f32[2,16,64,256]{3,2,1,0:T(8,128)S(1)} %fusion.33, ...), kind=kOutput, calls=%fused_computation.38 | convolution fusion | flops 287309312 | bytes 8030336 | tf_op jit(solution)/shard_map/gjtu,ugjp->tgjp/dot_general | solution.py:117
  88.4 2.8 mul.376
  91.2 2.9 copy.73
  94.1 3.9 %multiply_convert_fusion.2 = bf16[1,256,2048]{2,1,0:T(8,128)(2,1)} fusion(f32[1,256,2048]{2,1,0:T(8,128)} %mul.376, f32[1,256,2048]{2,1,0:T(8,128)} %copy.73, bf16[1,256,2048]{2,1,0:T(8,128)(2,1)S(1)} %copy-done, f32[2048]{0:T(1024)S(1)} %bitcast.117), kind=kLoop, calls=%fused_computation.37 | loop fusion | flops 4718592 | bytes 6299648 | tf_op jit(solution)/shard_map/convert_element_type | solution.py:137
  98.1 1.5 collective-permute-start.1
  99.5 2.8 mul.369
  102.4 3.1 %copy.70 = f32[1,1,256,2048]{3,2,1,0:T(8,128)} copy(f32[1,1,256,2048]{2,3,1,0:T(8,128)} %bitcast.99) | data formatting | bytes 4194304 | tf_op jit(solution)/shard_map/reshape | solution.py:135
  105.4 2.3 fusion.26
  107.8 15.4 %collective-permute-done.1 = bf16[1,256,2048]{2,1,0:T(8,128)(2,1)} collective-permute-done((bf16[1,256,2048]{2,1,0:T(8,128)(2,1)}, bf16[1,256,2048]{2,1,0:T(8,128)(2,1)}, u32[]{:S(2)}, u32[]{:S(2)}) %collective-permute-start.1) | collective-permute-done | bytes 1048608 | tf_op jit(solution)/shard_map/ppermute | solution.py:21
  124.5 2.1 fusion.28
  126.6 1.5 collective-permute-start.2
  128.1 45.2 %collective-permute-done.2 = bf16[2,256,2048]{2,1,0:T(8,128)(2,1)} collective-permute-done((bf16[2,256,2048]{2,1,0:T(8,128)(2,1)}, bf16[2,256,2048]{2,1,0:T(8,128)(2,1)}, u32[]{:S(2)}, u32[]{:S(2)}) %collective-permute-start.2) | collective-permute-done | bytes 2097184 | tf_op jit(solution)/shard_map/ppermute | solution.py:21
  173.3 2.1 pad_maximum_fusion
  177.8 10.4 %fusion.9 = bf16[1024,2048]{1,0:T(8,128)(2,1)} fusion(bf16[1024,2048]{1,0:T(8,128)(2,1)S(1)} %bitcast.101, bf16[1,2048,2048]{2,1,0:T(8,128)(2,1)S(1)} %bitcast.138), kind=kOutput, calls=%fused_computation.12 | convolution fusion | flops 8592031744 | bytes 16777216 | tf_op jit(solution)/shard_map/dot_general | solution.py:139
  188.2 77.0 %reduce-scatter.2.cloned.1.call-done = bf16[4,64,2048]{2,1,0:T(8,128)(2,1)} async-done(((bf16[4,256,2048]{2,1,0:T(8,128)(2,1)}), bf16[4,64,2048]{2,1,0:T(8,128)(2,1)}) %reduce-scatter.2.cloned.1.call-update) | async-done | bytes 1048592 | tf_op jit(solution)/shard_map/reduce_scatter | solution.py:144
  265.2 17.6 %all_to_all.15 = bf16[4,64,2048]{2,1,0:T(8,128)(2,1)S(1)} all-to-all(bf16[4,64,2048]{2,1,0:T(8,128)(2,1)} %reduce-scatter.2.cloned.1.call-done), channel_id=1, replica_groups=mesh['section'=2,'seq'=4,'head'=4] {'seq'}, dimensions={0} | all-to-all | bytes 2097152 | tf_op jit(solution)/shard_map/all_to_all | solution.py:145
  284.3 2.6 collective-permute-done.3
  (72 shorter events, 20.4 us)
Async XLA Ops:
  6.5 16.9 %copy-start.3 = (bf16[1,256,2048]{2,1,0:T(8,128)(2,1)S(1)}, bf16[1,256,2048]{2,1,0:T(8,128)(2,1)}, u32[]{:S(2)}) copy-start(bf16[1,256,2048]{2,1,0:T(8,128)(2,1)} %param.13) | copy-start | bytes 3145732
  6.5 73.4 %all-gather.4.cloned.1.call-start = ((), (), s32[]{:S(2)}) async-start(), calls=%async_computation.3 | async-start | bytes 5242880 | tf_op jit(solution)/shard_map/all_gather | solution.py:41
  8.1 13.2 %collective-permute-start = (bf16[3,3072]{1,0:T(4,128)(2,1)S(1)}, bf16[3,3072]{1,0:T(4,128)(2,1)S(1)}, u32[]{:S(2)}, u32[]{:S(2)}) collective-permute-start(bf16[3,3072]{1,0:T(4,128)(2,1)S(1)} %pad_maximum_fusion.5), channel_id=1, source_target_pairs={{0,4},{4,8},{8,12},{1,5},{5,9},{9,13},{2,6},{6,10},{10,14},{3,7},{... | collective-permute-start | bytes 55304 | tf_op jit(solution)/shard_map/ppermute | solution.py:35
  25.4 1.6 copy-start.8
  25.4 2.2 copy-start
  26.9 10.5 %copy-start.7 = (f32[1,4,512]{2,1,0:T(4,128)S(1)}, f32[1,4,512]{2,1,0:T(4,128)}, u32[]{:S(2)}) copy-start(f32[1,4,512]{2,1,0:T(4,128)} %param.20) | copy-start | bytes 24580
  26.9 10.6 %copy-start.4 = (bf16[1,256,512]{2,1,0:T(8,128)(2,1)S(1)}, bf16[1,256,512]{2,1,0:T(8,128)(2,1)}, u32[]{:S(2)}) copy-start(bf16[1,256,512]{2,1,0:T(8,128)(2,1)} %param.15) | copy-start | bytes 786436
  26.9 238.3 %reduce-scatter.2.cloned.1.call-start = ((), (), s32[]{:S(2)}) async-start(), calls=%async_computation.2 | async-start | bytes 5242880 | tf_op jit(solution)/shard_map/reduce_scatter | solution.py:144
  80.0 3.0 %copy-start.2 = (f32[1,256,2048]{1,2,0:T(8,128)S(1)}, f32[1,256,2048]{1,2,0:T(8,128)}, u32[]{:S(2)}) copy-start(f32[1,256,2048]{1,2,0:T(8,128)} %copy.71) | copy-start | bytes 6291460
  80.0 3.0 %copy-start.6 = (f32[256,2,16]{0,2,1:T(8,128)S(1)}, f32[256,2,16]{0,2,1:T(8,128)}, u32[]{:S(2)}) copy-start(f32[256,2,16]{0,2,1:T(8,128)} %get-tuple-element.9) | copy-start | bytes 98308
  91.2 2.9 copy-start.5
  98.1 25.1 %collective-permute-start.1 = (bf16[1,256,2048]{2,1,0:T(8,128)(2,1)}, bf16[1,256,2048]{2,1,0:T(8,128)(2,1)}, u32[]{:S(2)}, u32[]{:S(2)}) collective-permute-start(bf16[1,256,2048]{2,1,0:T(8,128)(2,1)} %multiply_convert_fusion.2), channel_id=1, source_target_pairs={{0,4},{4,0},{8,12},{12,8},{1,5},{5,1},{9,13},{13,9},{2,6},{6,2},{1... | collective-permute-start | bytes 3145736 | tf_op jit(solution)/shard_map/ppermute | solution.py:21
  102.4 3.1 %copy-start.1 = (f32[1,1,256,2048]{3,2,1,0:T(8,128)S(1)}, f32[1,1,256,2048]{3,2,1,0:T(8,128)}, u32[]{:S(2)}) copy-start(f32[1,1,256,2048]{3,2,1,0:T(8,128)} %mul.369) | copy-start | bytes 6291460
  126.6 46.7 %collective-permute-start.2 = (bf16[2,256,2048]{2,1,0:T(8,128)(2,1)}, bf16[2,256,2048]{2,1,0:T(8,128)(2,1)}, u32[]{:S(2)}, u32[]{:S(2)}) collective-permute-start(bf16[2,256,2048]{2,1,0:T(8,128)(2,1)} %get-tuple-element.8), channel_id=1, source_target_pairs={{0,8},{4,12},{8,0},{12,4},{1,9},{5,13},{9,1},{13,5},{2,10},{6,14},... | collective-permute-start | bytes 6291464 | tf_op jit(solution)/shard_map/ppermute | solution.py:21
  173.3 3.5 %slice-start = ((s8[8388608]{0:T(1024)(128)(4,1)}), s8[4194304]{0:T(1024)(128)(4,1)S(1)}, s32[]{:S(2)}) async-start(s8[8388608]{0:T(1024)(128)(4,1)} %bitcast.137), calls=%async_computation.4 | async-start | bytes 8388608
  175.4 2.4 slice-start.1
  284.2 2.7 collective-permute-start.3
Sparse Core Ops, SparseCore 0:
  27.0 52.8 all-gather.3
  188.3 76.7 reduce-scatter.1
